TPU v7x, 32 devices: a whole 2x2x4 slice. The times are simulated.
32 devices in a mesh: grp: 2 (over x), row: 16 (over z, y, core).
Axes of the slice: x: 2, y: 2, z: 4, core: 2. Of those that a mesh axis runs over, the one named last changes fastest.
Arguments:
- alignment: bfloat16 [128, 128, 256], P(('grp', 'row')), parts along dimension 0, may hold values from -6 to 6
- seq_flags: int32 [128], P(('grp', 'row')), parts along dimension 0, may hold values 0 or 1
- crop_flags: int32 [256], P('grp'), parts along dimension 0, may hold values 0 or 1
- norm_gain: float32 [256], replicated, may hold values from 0.5 to 1.5
- norm_bias: float32 [256], replicated, may hold values from -3 to 3
- left_weight: bfloat16 [256, 32], replicated, may hold values from -0.375 to 0.375
- left_bias: float32 [32], replicated, may hold values from -3 to 3
- right_weight: bfloat16 [256, 32], replicated, may hold values from -0.375 to 0.375
- right_bias: float32 [32], replicated, may hold values from -3 to 3
- out_weight: bfloat16 [1024, 128], replicated, may hold values from -0.1875 to 0.1875
- out_bias: float32 [128], replicated, may hold values from -3 to 3
Outputs:
- pair_update: bfloat16 [256, 128, 128], P(('grp', 'row')), parts along dimension 0
There are 2 independent parts, one for each index of `grp`. A program takes and returns all parts, laid end to end along the dimension named above; an argument that names none is the same for every part. Nothing has to cross between parts.
All inputs are finite; a program needn't handle non-finite values. No bound on the sum of `seq_flags` on one device may be relied on, other than what follows from the above.
Results may differ from a plain program's by a relative error of at most 0.004.
Values may be sent and summed in bfloat16 or wider, within the bound.
No kernel may reach another device: no remote copies, remote signals or barrier semaphores. Data moves between devices by JAX's collectives and lax.ppermute only.
A program may use at most 128 MiB of HBM per device.

v0:
```python
import jax
import jax.numpy as jnp
from jax import lax
from jax.sharding import PartitionSpec as P


def normalize(values, norm_gain, norm_bias):
    values = values.astype(jnp.float32)
    average = jnp.mean(values, axis=-1, keepdims=True)
    variance = jnp.mean((values - average) ** 2, axis=-1, keepdims=True)
    return (values - average) * lax.rsqrt(variance + 1e-05) * norm_gain + norm_bias


def project(normed, weight, bias, scaling):
    product = jnp.einsum(
        "src,cd->srd", normed, weight.astype(jnp.float32), precision=lax.Precision.HIGHEST
    )
    return ((product + bias) * scaling).astype(jnp.bfloat16)


def pair_tile(
    left_flat, column_piece, crop_rows, crop_cols, live_count, out_weight, out_bias, channels
):
    rows_here = crop_rows.shape[0]
    width_cols = column_piece.shape[1] // channels
    sums = lax.dot_general(
        left_flat, column_piece, (((0,), (0,)), ((), ())), preferred_element_type=jnp.float32
    )
    outer_sum = sums.reshape(rows_here, channels, width_cols, channels).transpose(0, 2, 1, 3)
    outer_sum = outer_sum.reshape(rows_here * width_cols, channels * channels).astype(jnp.bfloat16)
    projected = jnp.dot(outer_sum, out_weight, preferred_element_type=jnp.float32)
    projected = projected.reshape(rows_here, width_cols, out_weight.shape[1])
    divisor = jnp.maximum(live_count * crop_rows[:, None] * crop_cols[None, :], 1.0)
    return (projected / divisor[:, :, None] + out_bias).astype(jnp.bfloat16)


def column_blocks(
    left_flat, column_piece, crop_rows, crop_cols, live_count, out_weight, out_bias, channels
):
    rows_here = crop_rows.shape[0]
    width_cols = column_piece.shape[1] // channels
    span = max(1, 2048 // rows_here)
    if width_cols > span and width_cols % span == 0:

        def one_block(block_index):
            start = block_index * span
            piece_block = lax.dynamic_slice_in_dim(
                column_piece, start * channels, span * channels, 1
            )
            crop_block = lax.dynamic_slice_in_dim(crop_cols, start, span, 0)
            return pair_tile(
                left_flat,
                piece_block,
                crop_rows,
                crop_block,
                live_count,
                out_weight,
                out_bias,
                channels,
            )

        stacked = lax.map(one_block, jnp.arange(width_cols // span, dtype=jnp.int32))
        return stacked.transpose(1, 0, 2, 3).reshape(rows_here, width_cols, out_weight.shape[1])
    return pair_tile(
        left_flat, column_piece, crop_rows, crop_cols, live_count, out_weight, out_bias, channels
    )


def per_device(
    alignment,
    seq_flags,
    crop_flags,
    norm_gain,
    norm_bias,
    left_weight,
    left_bias,
    right_weight,
    right_bias,
    out_weight,
    out_bias,
):
    channels = left_weight.shape[1]
    devices_row = lax.axis_size("row")
    residues = alignment.shape[1]
    rows_here = residues // devices_row
    crop_float = crop_flags.astype(jnp.float32)
    my_index = lax.axis_index("row")
    crop_rows = lax.dynamic_slice_in_dim(crop_float, my_index * rows_here, rows_here, 0)
    regrouped = lax.all_to_all(alignment, "row", split_axis=1, concat_axis=0, tiled=True)
    all_flags = lax.all_gather(seq_flags, "row", axis=0, tiled=True)
    flag_float = all_flags.astype(jnp.float32)
    live_count = jnp.sum(flag_float)
    normed = normalize(regrouped, norm_gain, norm_bias)
    scaling = flag_float[:, None, None] * crop_rows[None, :, None]
    left = project(normed, left_weight, left_bias, scaling)
    right = project(normed, right_weight, right_bias, scaling)
    sequences = left.shape[0]
    left_flat = left.reshape(sequences, rows_here * channels)
    right_flat = right.reshape(sequences, rows_here * channels)
    return column_blocks(
        left_flat,
        lax.all_gather(right_flat, "row", axis=1, tiled=True),
        crop_rows,
        crop_float,
        live_count,
        out_weight,
        out_bias,
        channels,
    )


def solution(mesh):
    return jax.shard_map(
        per_device,
        mesh=mesh,
        in_specs=(
            P(("grp", "row"), None, None),
            P(("grp", "row")),
            P("grp"),
            P(),
            P(),
            P(),
            P(),
            P(),
            P(),
            P(),
            P(),
        ),
        out_specs=P(("grp", "row"), None, None),
        check_vma=False,
    )
```

profile of v0, /device:TPU:0, one launch (start us, length us, event | category | flops | bytes accessed | tf_op | source)
XLA Modules:
  0.0 54.4 jit_solution(9916558976857848131)
XLA Ops:
  0.0 1.9 %copy.75 = bf16[4,128,256]{2,0,1:T(4,128)(2,1)} copy(bf16[4,128,256]{2,1,0:T(8,128)(2,1)} %param.11) | data formatting | bytes 524288 | tf_op args[0]
  1.9 7.4 %all-to-all-start = ((bf16[4,128,256]{2,0,1:T(4,128)(2,1)}), bf16[4,128,256]{2,0,1:T(4,128)(2,1)S(1)}, u32[]{:S(2)}, u32[]{:S(2)}) async-start(bf16[4,128,256]{2,0,1:T(4,128)(2,1)} %copy.75), calls=%async_computation | async-start | bytes 524288 | tf_op jit(solution)/shard_map/all_to_all | solution.py:89
  9.4 1.3 %dynamic-slice = u32[1]{0:T(128)} dynamic-slice(u32[32]{0:T(128)} %constant.24, u32[]{:T(128)S(6)} %add.58), dynamic_slice_sizes={1} | dynamic-slice | bytes 12
  11.4 0.9 %dynamic-update-slice = s32[64]{0:T(128)S(1)} dynamic-update-slice(s32[64]{0:T(128)S(1)} %broadcast.80, s32[4]{0:T(128)} %param.12, u32[]{:T(128)} %bitcast.7) | dynamic-update-slice | bytes 36
  12.2 12.4 %all-reduce = s32[64]{0:T(128)S(1)} all-reduce(s32[64]{0:T(128)S(1)} %dynamic-update-slice), channel_id=1, replica_groups=mesh['grp'=2,'row'=16] {'row'}, use_global_device_ids=true, to_apply=%add | all-reduce | flops 64 | bytes 512
  24.7 0.7 %convert_reduce_fusion = f32[]{:T(128)} fusion(s32[64]{0:T(128)S(1)} %all-reduce), kind=kLoop, calls=%fused_computation.27 | loop fusion | flops 127 | bytes 260 | tf_op jit(solution)/shard_map/reduce_sum | solution.py:92
  25.4 0.7 %convert_element_type.51 = f32[128]{0:T(128)S(1)} convert(s32[128]{0:T(128)} %param.13) | non-fusion elementwise | flops 128 | bytes 1024 | tf_op jit(solution)/shard_map/convert_element_type | solution.py:86
  26.0 0.8 %broadcast_multiply_fusion.2 = (f32[8]{0:T(128)S(1)}, f32[8]{0:T(128)S(1)}) fusion(f32[]{:T(128)} %convert_reduce_fusion, f32[128]{0:T(128)S(1)} %convert_element_type.51, s32[]{:T(128)S(6)} %select_n.3), kind=kLoop, calls=%fused_computation.26 | loop fusion | flops 8 | bytes 104 | tf_op jit(solution)/shard_map/mul | solution.py:33
  26.8 0.1 multiply_maximum_fusion
  26.9 0.1 fusion.10
  27.2 0.1 copy.81
  27.2 0.1 copy.80
  27.3 0.3 multiply_reduce_fusion
  27.7 0.1 copy.84
  27.9 0.2 fusion.9
  28.2 0.4 fusion.5
  28.5 0.1 copy.86
  28.7 21.0 %all_gather.7 = bf16[64,4096]{0,1:T(8,128)(2,1)S(1)} all-gather(bf16[64,256]{0,1:T(8,128)(2,1)S(1)} %bitcast.57), channel_id=1, replica_groups=mesh['grp'=2,'row'=16] {'row'}, dimensions={1}, use_global_device_ids=true | all-gather | bytes 557056 | tf_op jit(solution)/shard_map/all_gather | solution.py:102
  49.7 1.1 %copy.87 = bf16[128,32,64]{0,2,1:T(8,128)(2,1)S(1)} copy(bf16[128,32,64]{2,1,0:T(8,128)(2,1)S(1)} %bitcast.55) | data formatting | bytes 1048576 | tf_op jit(solution)/shard_map/dot_general | solution.py:26
  50.8 0.4 fusion.4
  51.2 0.1 copy.85
  51.3 0.7 %convert_bitcast_fusion = bf16[8,128,32,32]{1,2,3,0:T(8,128)(2,1)S(1)} fusion(bf16[128,32,64]{0,2,1:T(8,128)(2,1)S(1)} %copy.87, bf16[64,8,32]{0,2,1:T(8,128)(2,1)S(1)} %copy.85), kind=kOutput, calls=%fused_computation | convolution fusion | flops 135266304 | bytes 2654208 | tf_op jit(solution)/shard_map/dot_general | solution.py:26
  52.0 0.8 %copy.88 = bf16[8,128,32,32]{1,3,2,0:T(8,128)(2,1)S(1)} copy(bf16[8,128,32,32]{1,2,3,0:T(8,128)(2,1)S(1)} %convert_bitcast_fusion) | data formatting | bytes 4194304 | tf_op jit(solution)/shard_map/convert_element_type | solution.py:30
  52.9 1.5 %fusion.1 = bf16[8,128,128]{2,1,0:T(8,128)(2,1)} fusion(bf16[8,128,1024]{1,2,0:T(8,128)(2,1)S(1)} %bitcast.56, bf16[1024,128]{1,0:T(8,128)(2,1)S(1)} %copy-done, f32[128]{0:T(128)S(1)} %copy-done.7, f32[8,128]{1,0:T(8,128)S(1)} %multiply_maximum_fusion), kind=kOutput, calls=%fused_computation.3 | convolution fusion | flops 268828672 | bytes 2626048 | tf_op jit(solution)/shard_map/dot_general | solution.py:31
  (26 shorter events, 0.4 us)
Async XLA Ops:
  0.0 52.9 %copy-start = (bf16[1024,128]{1,0:T(8,128)(2,1)S(1)}, bf16[1024,128]{1,0:T(8,128)(2,1)}, u32[]{:S(2)}) copy-start(bf16[1024,128]{1,0:T(8,128)(2,1)} %param.20) | copy-start | bytes 786436
  0.0 27.9 %copy-start.4 = (f32[256]{0:T(256)S(1)}, f32[256]{0:T(256)}, u32[]{:S(2)}) copy-start(f32[256]{0:T(256)} %param.14) | copy-start | bytes 3076
  0.0 27.9 %copy-start.3 = (f32[256]{0:T(256)S(1)}, f32[256]{0:T(256)}, u32[]{:S(2)}) copy-start(f32[256]{0:T(256)} %param.15) | copy-start | bytes 3076
  1.9 25.0 %all-to-all-start = ((bf16[4,128,256]{2,0,1:T(4,128)(2,1)}), bf16[4,128,256]{2,0,1:T(4,128)(2,1)S(1)}, u32[]{:S(2)}, u32[]{:S(2)}) async-start(bf16[4,128,256]{2,0,1:T(4,128)(2,1)} %copy.75), calls=%async_computation | async-start | bytes 524288 | tf_op jit(solution)/shard_map/all_to_all | solution.py:89
  9.3 18.8 %copy-start.1 = (bf16[256,32]{0,1:T(8,128)(2,1)S(1)}, bf16[256,32]{0,1:T(8,128)(2,1)}, u32[]{:S(2)}) copy-start(bf16[256,32]{0,1:T(8,128)(2,1)} %param.18) | copy-start | bytes 49156
  9.3 18.8 %copy-start.5 = (f32[32]{0:T(128)S(1)}, f32[32]{0:T(128)}, u32[]{:S(2)}) copy-start(f32[32]{0:T(128)} %param.19) | copy-start | bytes 388
  27.9 22.9 %copy-start.2 = (bf16[256,32]{0,1:T(8,128)(2,1)S(1)}, bf16[256,32]{0,1:T(8,128)(2,1)}, u32[]{:S(2)}) copy-start(bf16[256,32]{0,1:T(8,128)(2,1)} %param.16) | copy-start | bytes 49156
  27.9 22.9 %copy-start.6 = (f32[32]{0:T(128)S(1)}, f32[32]{0:T(128)}, u32[]{:S(2)}) copy-start(f32[32]{0:T(128)} %param.17) | copy-start | bytes 388
  52.0 0.8 %copy-start.7 = (f32[128]{0:T(128)S(1)}, f32[128]{0:T(128)}, u32[]{:S(2)}) copy-start(f32[128]{0:T(128)} %param.21) | copy-start | bytes 1540
where the time goes:
time: 54.7 us; the launch traced here: 54.4 us
  blocking collectives  33.5 us (61%)
  starting transfers between devices  7.42 us (14%)
  local copies, waits for them, and re-layouts  6.75 us (12%)
  other arithmetic  2.94 us (5%)
  matrix products  2.91 us (5%)
  between operations  0.9 us (2%)
    all_gather x1, blocking collectives, per_device(): lax.all_gather(right_flat, 'row', axis=1, tiled=True)  21 us
    unnamed x1, blocking collectives  12.4 us
    all_to_all x1, starting transfers between devices, per_device(): lax.all_to_all(alignment, 'row', split_axis=1, concat_axis=0, tiled=True)  7.42 us
    unnamed x20, local copies, waits for them, and re-layouts  4.12 us
    dot_general x1, matrix products, pair_tile(): jnp.dot(outer_sum, out_weight, preferred_element_type=jnp.float32)  1.49 us
    dot_general x1, local copies, waits for them, and re-layouts, pair_tile(): lax.dot_general(left_flat, column_piece, (((0,), (0,)), ((), ())), prefer...  1.11 us
  transfers between devices with their start and end apart: 1, of which 0 were waited for; matrix products, arithmetic and copies ran while one was open for 8% of the time, Pallas kernels for 0%

commit v1 on v0

--- a/solution.py
+++ b/solution.py
@@ -2,6 +2,28 @@
 import jax.numpy as jnp
 from jax import lax
 from jax.sharding import PartitionSpec as P
+
+
+def cut_along(x, dim, length):
+    before, after = (x.shape[:dim], x.shape[dim + 1 :])
+    return jnp.moveaxis(x.reshape(*before, length, -1, *after), dim, 0)
+
+
+def laid_out(blocks, dim):
+    blocks = jnp.moveaxis(blocks, 0, dim)
+    shape = blocks.shape
+    return blocks.reshape(*shape[:dim], shape[dim] * shape[dim + 1], *shape[dim + 2 :])
+
+
+def swapped_with_each(shard, axis, split_dim, concat_dim):
+    size, here = (lax.axis_size(axis), lax.axis_index(axis))
+    blocks = cut_along(shard, split_dim, size)
+    done = [blocks[here]]
+    for step in range(1, size):
+        sent = blocks[here ^ step]
+        done.append(lax.ppermute(sent, axis, [(i, i ^ step) for i in range(size)]))
+    blocks = jnp.stack(done)[here ^ jnp.arange(size)]
+    return laid_out(blocks, concat_dim)
 
 
 def normalize(values, norm_gain, norm_bias):
@@ -86,7 +108,7 @@
     crop_float = crop_flags.astype(jnp.float32)
     my_index = lax.axis_index("row")
     crop_rows = lax.dynamic_slice_in_dim(crop_float, my_index * rows_here, rows_here, 0)
-    regrouped = lax.all_to_all(alignment, "row", split_axis=1, concat_axis=0, tiled=True)
+    regrouped = swapped_with_each(alignment, "row", 1, 0)
     all_flags = lax.all_gather(seq_flags, "row", axis=0, tiled=True)
     flag_float = all_flags.astype(jnp.float32)
     live_count = jnp.sum(flag_float)

time: 54.7 us -> 74 us (1.35)
  starting transfers between devices: 7.42 us -> 20 us
  waiting for transfers between devices: 0.01 us -> 4.04 us
  blocking collectives: 33.5 us -> 36.3 us
    ppermute x0 -> x15, starting transfers between devices: none -> 20 us  [swapped_with_each(): done.append(lax.ppermute(sent, axis, [(i, i ^ step) for i in range(size)]))]
    all_to_all x1 -> x0, starting transfers between devices: 7.42 us -> none  [per_device(): lax.all_to_all(alignment, 'row', split_axis=1, concat_axis=0, tiled=True)]
    ppermute x0 -> x15, waiting for transfers between devices: none -> 4.04 us  [swapped_with_each(): done.append(lax.ppermute(sent, axis, [(i, i ^ step) for i in range(size)]))]
    all_gather x1, blocking collectives: 21 us -> 23.9 us  [per_device(): lax.all_gather(right_flat, 'row', axis=1, tiled=True)]
    unnamed x20 -> x34, local copies, waits for them, and re-layouts: 4.12 us -> 2.89 us
    squeeze x0 -> x1, local copies, waits for them, and re-layouts: none -> 0.97 us  [swapped_with_each(): sent = blocks[here ^ step]]
  transfers between devices with their start and end apart: 1 -> 15, of which waited for: 0 -> 2; matrix products, arithmetic and copies ran while one was open for 8% -> 7% of each run, Pallas kernels for 0% -> 0%
where the time goes in v1:
time: 74 us; the launch traced here: 73.8 us
  blocking collectives  36.3 us (49%)
  starting transfers between devices  20 us (27%)
  local copies, waits for them, and re-layouts  6.62 us (9%)
  waiting for transfers between devices  4.04 us (5%)
  matrix products  2.91 us (4%)
  other arithmetic  2.82 us (4%)
  between operations  0.99 us (1%)
    all_gather x1, blocking collectives, per_device(): lax.all_gather(right_flat, 'row', axis=1, tiled=True)  23.9 us
    ppermute x15, starting transfers between devices, swapped_with_each(): done.append(lax.ppermute(sent, axis, [(i, i ^ step) for i in range(size)]))  20 us
    unnamed x1, blocking collectives  12.4 us
    ppermute x15, waiting for transfers between devices, swapped_with_each(): done.append(lax.ppermute(sent, axis, [(i, i ^ step) for i in range(size)]))  4.04 us
    unnamed x34, local copies, waits for them, and re-layouts  2.89 us
    dot_general x1, matrix products, pair_tile(): jnp.dot(outer_sum, out_weight, preferred_element_type=jnp.float32)  1.49 us
  transfers between devices with their start and end apart: 15, of which 2 were waited for; matrix products, arithmetic and copies ran while one was open for 7% of the time, Pallas kernels for 0%

profile of v1, /device:TPU:0, one launch (start us, length us, event | category | flops | bytes accessed | tf_op | source)
XLA Modules:
  0.0 73.8 jit_solution(9586829825203199771)
XLA Ops:
  0.1 1.0 %dynamic-slice_bitcast_fusion = (bf16[4,8,256]{2,1,0:T(8,128)(2,1)S(1)}, bf16[4,8,256]{2,1,0:T(8,128)(2,1)S(1)}, bf16[4,8,256]{2,1,0:T(8,128)(2,1)S(1)}, bf16[4,...) fusion(bf16[4,16,8,256]{3,2,1,0:T(8,128)(2,1)} %bitcast.113, ...), kind=kLoop, calls=%fused_computation.41 | loop fusion | bytes 491580 | tf_op jit(solution)/shard_map/squeeze | solution.py:23
  1.6 2.6 %collective-permute-start.1 = (bf16[4,8,256]{2,1,0:T(8,128)(2,1)S(1)}, bf16[4,8,256]{2,1,0:T(8,128)(2,1)S(1)}, u32[]{:S(2)}, u32[]{:S(2)}) collective-permute-start(bf16[4,8,256]{2,1,0:T(8,128)(2,1)S(1)} %get-tuple-element.20), channel_id=1, source_target_pairs={{0,2},{1,3},{2,0},{3,1},{4,6},{5,7},{6,4},{7,5},{8,10},{9,11},{10,... | collective-permute-start | bytes 49160 | tf_op jit(solution)/shard_map/ppermute | solution.py:24
  4.3 1.8 %collective-permute-start.3 = (bf16[4,8,256]{2,1,0:T(8,128)(2,1)S(1)}, bf16[4,8,256]{2,1,0:T(8,128)(2,1)S(1)}, u32[]{:S(2)}, u32[]{:S(2)}) collective-permute-start(bf16[4,8,256]{2,1,0:T(8,128)(2,1)S(1)} %get-tuple-element.18), channel_id=1, source_target_pairs={{0,4},{1,5},{2,6},{3,7},{4,0},{5,1},{6,2},{7,3},{8,12},{9,13},{10,... | collective-permute-start | bytes 49160 | tf_op jit(solution)/shard_map/ppermute | solution.py:24
  6.1 1.2 %dynamic-slice.64 = u32[1]{0:T(128)} dynamic-slice(u32[32]{0:T(128)} %constant.56, u32[]{:T(128)S(6)} %add.133), dynamic_slice_sizes={1} | dynamic-slice | bytes 12
  8.0 0.9 %dynamic-update-slice = s32[64]{0:T(128)S(1)} dynamic-update-slice(s32[64]{0:T(128)S(1)} %broadcast.109, s32[4]{0:T(128)} %param.12, u32[]{:T(128)} %bitcast.37) | dynamic-update-slice | bytes 36
  8.8 12.4 %all-reduce = s32[64]{0:T(128)S(1)} all-reduce(s32[64]{0:T(128)S(1)} %dynamic-update-slice), channel_id=1, replica_groups=mesh['grp'=2,'row'=16] {'row'}, use_global_device_ids=true, to_apply=%add | all-reduce | flops 64 | bytes 512
  21.2 0.6 convert_reduce_fusion.1
  21.8 0.7 constant_dynamic-update-slice_fusion.15
  22.6 0.7 convert_element_type.41
  23.2 0.7 broadcast_multiply_fusion.2
  24.1 0.8 %collective-permute-start.5 = (bf16[4,8,256]{2,1,0:T(8,128)(2,1)S(1)}, bf16[4,8,256]{2,1,0:T(8,128)(2,1)S(1)}, u32[]{:S(2)}, u32[]{:S(2)}) collective-permute-start(bf16[4,8,256]{2,1,0:T(8,128)(2,1)S(1)} %get-tuple-element.16), channel_id=1, source_target_pairs={{0,6},{1,7},{2,4},{3,5},{4,2},{5,3},{6,0},{7,1},{8,14},{9,15},{10,... | collective-permute-start | bytes 49160 | tf_op jit(solution)/shard_map/ppermute | solution.py:24
  25.4 4.1 %collective-permute-start.8 = (bf16[4,8,256]{2,1,0:T(8,128)(2,1)S(1)}, bf16[4,8,256]{2,1,0:T(8,128)(2,1)S(1)}, u32[]{:S(2)}, u32[]{:S(2)}) collective-permute-start(bf16[4,8,256]{2,1,0:T(8,128)(2,1)S(1)} %get-tuple-element.13), channel_id=1, source_target_pairs={{0,9},{1,8},{2,11},{3,10},{4,13},{5,12},{6,15},{7,14},{8,1},{9,0},... | collective-permute-start | bytes 49160 | tf_op jit(solution)/shard_map/ppermute | solution.py:24
  29.5 0.7 collective-permute-start.9
  30.2 1.1 %collective-permute-start.10 = (bf16[4,8,256]{2,1,0:T(8,128)(2,1)S(1)}, bf16[4,8,256]{2,1,0:T(8,128)(2,1)S(1)}, u32[]{:S(2)}, u32[]{:S(2)}) collective-permute-start(bf16[4,8,256]{2,1,0:T(8,128)(2,1)S(1)} %get-tuple-element.11), channel_id=1, source_target_pairs={{0,11},{1,10},{2,9},{3,8},{4,15},{5,14},{6,13},{7,12},{8,3},{9,2},... | collective-permute-start | bytes 49160 | tf_op jit(solution)/shard_map/ppermute | solution.py:24
  31.2 1.8 %collective-permute-start.11 = (bf16[4,8,256]{2,1,0:T(8,128)(2,1)S(1)}, bf16[4,8,256]{2,1,0:T(8,128)(2,1)S(1)}, u32[]{:S(2)}, u32[]{:S(2)}) collective-permute-start(bf16[4,8,256]{2,1,0:T(8,128)(2,1)S(1)} %get-tuple-element.10), channel_id=1, source_target_pairs={{0,12},{1,13},{2,14},{3,15},{4,8},{5,9},{6,10},{7,11},{8,4},{9,5},... | collective-permute-start | bytes 49160 | tf_op jit(solution)/shard_map/ppermute | solution.py:24
  33.0 3.6 %collective-permute-start.12 = (bf16[4,8,256]{2,1,0:T(8,128)(2,1)S(1)}, bf16[4,8,256]{2,1,0:T(8,128)(2,1)S(1)}, u32[]{:S(2)}, u32[]{:S(2)}) collective-permute-start(bf16[4,8,256]{2,1,0:T(8,128)(2,1)S(1)} %get-tuple-element.9), channel_id=1, source_target_pairs={{0,13},{1,12},{2,15},{3,14},{4,9},{5,8},{6,11},{7,10},{8,5},{9,4},... | collective-permute-start | bytes 49160 | tf_op jit(solution)/shard_map/ppermute | solution.py:24
  36.6 0.7 collective-permute-start.13
  37.3 2.0 %collective-permute-start.14 = (bf16[4,8,256]{2,1,0:T(8,128)(2,1)S(1)}, bf16[4,8,256]{2,1,0:T(8,128)(2,1)S(1)}, u32[]{:S(2)}, u32[]{:S(2)}) collective-permute-start(bf16[4,8,256]{2,1,0:T(8,128)(2,1)S(1)} %get-tuple-element.7), channel_id=1, source_target_pairs={{0,15},{1,14},{2,13},{3,12},{4,11},{5,10},{6,9},{7,8},{8,7},{9,6},... | collective-permute-start | bytes 49160 | tf_op jit(solution)/shard_map/ppermute | solution.py:24
  39.3 3.8 %collective-permute-done.13 = bf16[4,8,256]{2,1,0:T(8,128)(2,1)S(1)} collective-permute-done((bf16[4,8,256]{2,1,0:T(8,128)(2,1)S(1)}, bf16[4,8,256]{2,1,0:T(8,128)(2,1)S(1)}, u32[]{:S(2)}, u32[]{:S(2)}) %collective-permute-start.13) | collective-permute-done | bytes 16416 | tf_op jit(solution)/shard_map/ppermute | solution.py:24
  45.2 23.9 %all_gather.7 = bf16[64,4096]{0,1:T(8,128)(2,1)S(1)} all-gather(bf16[64,256]{0,1:T(8,128)(2,1)S(1)} %bitcast.112), channel_id=1, replica_groups=mesh['grp'=2,'row'=16] {'row'}, dimensions={1}, use_global_device_ids=true | all-gather | bytes 557056 | tf_op jit(solution)/shard_map/all_gather | solution.py:124
  69.1 1.1 %copy.15 = bf16[128,32,64]{0,2,1:T(8,128)(2,1)S(1)} copy(bf16[128,32,64]{2,1,0:T(8,128)(2,1)S(1)} %bitcast.109) | data formatting | bytes 1048576 | tf_op jit(solution)/shard_map/dot_general | solution.py:48
  70.7 0.7 convert_bitcast_fusion
  71.4 0.8 %copy.16 = bf16[8,128,32,32]{1,3,2,0:T(8,128)(2,1)S(1)} copy(bf16[8,128,32,32]{1,2,3,0:T(8,128)(2,1)S(1)} %convert_bitcast_fusion) | data formatting | bytes 4194304 | tf_op jit(solution)/shard_map/convert_element_type | solution.py:52
  72.3 1.5 %fusion.1 = bf16[8,128,128]{2,1,0:T(8,128)(2,1)} fusion(bf16[8,128,1024]{1,2,0:T(8,128)(2,1)S(1)} %bitcast.110, bf16[1024,128]{1,0:T(8,128)(2,1)S(1)} %copy-done, f32[128]{0:T(128)S(1)} %copy-done.7, f32[8,128]{1,0:T(8,128)S(1)} %multiply_maximum_fusion), kind=kOutput, calls=%fused_computation.4 | convolution fusion | flops 268828672 | bytes 2626048 | tf_op jit(solution)/shard_map/dot_general | solution.py:53
  (66 shorter events, 3.7 us)
Async XLA Ops:
  0.0 72.3 %copy-start = (bf16[1024,128]{1,0:T(8,128)(2,1)S(1)}, bf16[1024,128]{1,0:T(8,128)(2,1)}, u32[]{:S(2)}) copy-start(bf16[1024,128]{1,0:T(8,128)(2,1)} %param.20) | copy-start | bytes 786436
  0.0 44.4 %copy-start.4 = (f32[256]{0:T(256)S(1)}, f32[256]{0:T(256)}, u32[]{:S(2)}) copy-start(f32[256]{0:T(256)} %param.14) | copy-start | bytes 3076
  0.0 44.4 %copy-start.3 = (f32[256]{0:T(256)S(1)}, f32[256]{0:T(256)}, u32[]{:S(2)}) copy-start(f32[256]{0:T(256)} %param.15) | copy-start | bytes 3076
  0.0 44.6 %copy-start.1 = (bf16[256,32]{0,1:T(8,128)(2,1)S(1)}, bf16[256,32]{0,1:T(8,128)(2,1)}, u32[]{:S(2)}) copy-start(bf16[256,32]{0,1:T(8,128)(2,1)} %param.18) | copy-start | bytes 49156
  0.0 44.6 %copy-start.5 = (f32[32]{0:T(128)S(1)}, f32[32]{0:T(128)}, u32[]{:S(2)}) copy-start(f32[32]{0:T(128)} %param.19) | copy-start | bytes 388
  1.1 23.0 %collective-permute-start = (bf16[4,8,256]{2,1,0:T(8,128)(2,1)S(1)}, bf16[4,8,256]{2,1,0:T(8,128)(2,1)S(1)}, u32[]{:S(2)}, u32[]{:S(2)}) collective-permute-start(bf16[4,8,256]{2,1,0:T(8,128)(2,1)S(1)} %get-tuple-element.21), channel_id=1, source_target_pairs={{0,1},{1,0},{2,3},{3,2},{4,5},{5,4},{6,7},{7,6},{8,9},{9,8},{10,11... | collective-permute-start | bytes 49160 | tf_op jit(solution)/shard_map/ppermute | solution.py:24
  1.6 23.3 %collective-permute-start.1 = (bf16[4,8,256]{2,1,0:T(8,128)(2,1)S(1)}, bf16[4,8,256]{2,1,0:T(8,128)(2,1)S(1)}, u32[]{:S(2)}, u32[]{:S(2)}) collective-permute-start(bf16[4,8,256]{2,1,0:T(8,128)(2,1)S(1)} %get-tuple-element.20), channel_id=1, source_target_pairs={{0,2},{1,3},{2,0},{3,1},{4,6},{5,7},{6,4},{7,5},{8,10},{9,11},{10,... | collective-permute-start | bytes 49160 | tf_op jit(solution)/shard_map/ppermute | solution.py:24
  4.2 20.7 %collective-permute-start.2 = (bf16[4,8,256]{2,1,0:T(8,128)(2,1)S(1)}, bf16[4,8,256]{2,1,0:T(8,128)(2,1)S(1)}, u32[]{:S(2)}, u32[]{:S(2)}) collective-permute-start(bf16[4,8,256]{2,1,0:T(8,128)(2,1)S(1)} %get-tuple-element.19), channel_id=1, source_target_pairs={{0,3},{1,2},{2,1},{3,0},{4,7},{5,6},{6,5},{7,4},{8,11},{9,10},{10,... | collective-permute-start | bytes 49160 | tf_op jit(solution)/shard_map/ppermute | solution.py:24
  4.3 21.1 %collective-permute-start.3 = (bf16[4,8,256]{2,1,0:T(8,128)(2,1)S(1)}, bf16[4,8,256]{2,1,0:T(8,128)(2,1)S(1)}, u32[]{:S(2)}, u32[]{:S(2)}) collective-permute-start(bf16[4,8,256]{2,1,0:T(8,128)(2,1)S(1)} %get-tuple-element.18), channel_id=1, source_target_pairs={{0,4},{1,5},{2,6},{3,7},{4,0},{5,1},{6,2},{7,3},{8,12},{9,13},{10,... | collective-permute-start | bytes 49160 | tf_op jit(solution)/shard_map/ppermute | solution.py:24
  6.1 23.4 %collective-permute-start.4 = (bf16[4,8,256]{2,1,0:T(8,128)(2,1)S(1)}, bf16[4,8,256]{2,1,0:T(8,128)(2,1)S(1)}, u32[]{:S(2)}, u32[]{:S(2)}) collective-permute-start(bf16[4,8,256]{2,1,0:T(8,128)(2,1)S(1)} %get-tuple-element.17), channel_id=1, source_target_pairs={{0,5},{1,4},{2,7},{3,6},{4,1},{5,0},{6,3},{7,2},{8,13},{9,12},{10,... | collective-permute-start | bytes 49160 | tf_op jit(solution)/shard_map/ppermute | solution.py:24
  24.1 6.0 %collective-permute-start.5 = (bf16[4,8,256]{2,1,0:T(8,128)(2,1)S(1)}, bf16[4,8,256]{2,1,0:T(8,128)(2,1)S(1)}, u32[]{:S(2)}, u32[]{:S(2)}) collective-permute-start(bf16[4,8,256]{2,1,0:T(8,128)(2,1)S(1)} %get-tuple-element.16), channel_id=1, source_target_pairs={{0,6},{1,7},{2,4},{3,5},{4,2},{5,3},{6,0},{7,1},{8,14},{9,15},{10,... | collective-permute-start | bytes 49160 | tf_op jit(solution)/shard_map/ppermute | solution.py:24
  24.9 6.3 %collective-permute-start.6 = (bf16[4,8,256]{2,1,0:T(8,128)(2,1)S(1)}, bf16[4,8,256]{2,1,0:T(8,128)(2,1)S(1)}, u32[]{:S(2)}, u32[]{:S(2)}) collective-permute-start(bf16[4,8,256]{2,1,0:T(8,128)(2,1)S(1)} %get-tuple-element.15), channel_id=1, source_target_pairs={{0,7},{1,6},{2,5},{3,4},{4,3},{5,2},{6,1},{7,0},{8,15},{9,14},{10,... | collective-permute-start | bytes 49160 | tf_op jit(solution)/shard_map/ppermute | solution.py:24
  25.0 8.1 %collective-permute-start.7 = (bf16[4,8,256]{2,1,0:T(8,128)(2,1)S(1)}, bf16[4,8,256]{2,1,0:T(8,128)(2,1)S(1)}, u32[]{:S(2)}, u32[]{:S(2)}) collective-permute-start(bf16[4,8,256]{2,1,0:T(8,128)(2,1)S(1)} %get-tuple-element.14), channel_id=1, source_target_pairs={{0,8},{1,9},{2,10},{3,11},{4,12},{5,13},{6,14},{7,15},{8,0},{9,1},... | collective-permute-start | bytes 49160 | tf_op jit(solution)/shard_map/ppermute | solution.py:24
  25.4 11.2 %collective-permute-start.8 = (bf16[4,8,256]{2,1,0:T(8,128)(2,1)S(1)}, bf16[4,8,256]{2,1,0:T(8,128)(2,1)S(1)}, u32[]{:S(2)}, u32[]{:S(2)}) collective-permute-start(bf16[4,8,256]{2,1,0:T(8,128)(2,1)S(1)} %get-tuple-element.13), channel_id=1, source_target_pairs={{0,9},{1,8},{2,11},{3,10},{4,13},{5,12},{6,15},{7,14},{8,1},{9,0},... | collective-permute-start | bytes 49160 | tf_op jit(solution)/shard_map/ppermute | solution.py:24
  29.5 7.8 %collective-permute-start.9 = (bf16[4,8,256]{2,1,0:T(8,128)(2,1)S(1)}, bf16[4,8,256]{2,1,0:T(8,128)(2,1)S(1)}, u32[]{:S(2)}, u32[]{:S(2)}) collective-permute-start(bf16[4,8,256]{2,1,0:T(8,128)(2,1)S(1)} %get-tuple-element.12), channel_id=1, source_target_pairs={{0,10},{1,11},{2,8},{3,9},{4,14},{5,15},{6,12},{7,13},{8,2},{9,3},... | collective-permute-start | bytes 49160 | tf_op jit(solution)/shard_map/ppermute | solution.py:24
  30.2 9.1 %collective-permute-start.10 = (bf16[4,8,256]{2,1,0:T(8,128)(2,1)S(1)}, bf16[4,8,256]{2,1,0:T(8,128)(2,1)S(1)}, u32[]{:S(2)}, u32[]{:S(2)}) collective-permute-start(bf16[4,8,256]{2,1,0:T(8,128)(2,1)S(1)} %get-tuple-element.11), channel_id=1, source_target_pairs={{0,11},{1,10},{2,9},{3,8},{4,15},{5,14},{6,13},{7,12},{8,3},{9,2},... | collective-permute-start | bytes 49160 | tf_op jit(solution)/shard_map/ppermute | solution.py:24
  31.2 8.0 %collective-permute-start.11 = (bf16[4,8,256]{2,1,0:T(8,128)(2,1)S(1)}, bf16[4,8,256]{2,1,0:T(8,128)(2,1)S(1)}, u32[]{:S(2)}, u32[]{:S(2)}) collective-permute-start(bf16[4,8,256]{2,1,0:T(8,128)(2,1)S(1)} %get-tuple-element.10), channel_id=1, source_target_pairs={{0,12},{1,13},{2,14},{3,15},{4,8},{5,9},{6,10},{7,11},{8,4},{9,5},... | collective-permute-start | bytes 49160 | tf_op jit(solution)/shard_map/ppermute | solution.py:24
  33.0 6.2 %collective-permute-start.12 = (bf16[4,8,256]{2,1,0:T(8,128)(2,1)S(1)}, bf16[4,8,256]{2,1,0:T(8,128)(2,1)S(1)}, u32[]{:S(2)}, u32[]{:S(2)}) collective-permute-start(bf16[4,8,256]{2,1,0:T(8,128)(2,1)S(1)} %get-tuple-element.9), channel_id=1, source_target_pairs={{0,13},{1,12},{2,15},{3,14},{4,9},{5,8},{6,11},{7,10},{8,5},{9,4},... | collective-permute-start | bytes 49160 | tf_op jit(solution)/shard_map/ppermute | solution.py:24
  36.6 6.5 %collective-permute-start.13 = (bf16[4,8,256]{2,1,0:T(8,128)(2,1)S(1)}, bf16[4,8,256]{2,1,0:T(8,128)(2,1)S(1)}, u32[]{:S(2)}, u32[]{:S(2)}) collective-permute-start(bf16[4,8,256]{2,1,0:T(8,128)(2,1)S(1)} %get-tuple-element.8), channel_id=1, source_target_pairs={{0,14},{1,15},{2,12},{3,13},{4,10},{5,11},{6,8},{7,9},{8,6},{9,7},... | collective-permute-start | bytes 49160 | tf_op jit(solution)/shard_map/ppermute | solution.py:24
  37.3 6.0 %collective-permute-start.14 = (bf16[4,8,256]{2,1,0:T(8,128)(2,1)S(1)}, bf16[4,8,256]{2,1,0:T(8,128)(2,1)S(1)}, u32[]{:S(2)}, u32[]{:S(2)}) collective-permute-start(bf16[4,8,256]{2,1,0:T(8,128)(2,1)S(1)} %get-tuple-element.7), channel_id=1, source_target_pairs={{0,15},{1,14},{2,13},{3,12},{4,11},{5,10},{6,9},{7,8},{8,7},{9,6},... | collective-permute-start | bytes 49160 | tf_op jit(solution)/shard_map/ppermute | solution.py:24
  44.4 25.8 %copy-start.2 = (bf16[256,32]{0,1:T(8,128)(2,1)S(1)}, bf16[256,32]{0,1:T(8,128)(2,1)}, u32[]{:S(2)}) copy-start(bf16[256,32]{0,1:T(8,128)(2,1)} %param.16) | copy-start | bytes 49156
  44.4 25.8 %copy-start.6 = (f32[32]{0:T(128)S(1)}, f32[32]{0:T(128)}, u32[]{:S(2)}) copy-start(f32[32]{0:T(128)} %param.17) | copy-start | bytes 388
  71.4 0.8 %copy-start.7 = (f32[128]{0:T(128)S(1)}, f32[128]{0:T(128)}, u32[]{:S(2)}) copy-start(f32[128]{0:T(128)} %param.21) | copy-start | bytes 1540
